TPU v7x, 32 devices: a whole 2x2x4 slice. The times are simulated.
32 devices in a mesh: dp: 4 (over y, x), tensor: 8 (over z, core).
Axes of the slice: x: 2, y: 2, z: 4, core: 2. Of those that a mesh axis runs over, the one named last changes fastest.
Arguments:
- tokens: bfloat16 [128, 4096], P(('dp', 'tensor')), may hold values from -6 to 6
- norm_gain: bfloat16 [4096], replicated, may hold values from 0.099609375 to 1.8984375
- gate_weight: bfloat16 [4096, 14336], P(None, 'tensor'), may hold values from -0.09375 to 0.09375
- up_weight: bfloat16 [4096, 14336], P(None, 'tensor'), may hold values from -0.09375 to 0.09375
- down_weight: bfloat16 [14336, 4096], P('tensor'), may hold values from -0.046875 to 0.046875
- drop_mask: int32 [128, 4096], P(('dp', 'tensor')), may hold values 0 or 1
- grad_bucket: bfloat16 [4, 2048, 512], P('dp', 'tensor'), may hold values from -6 to 6
Outputs:
- mixed: bfloat16 [128, 4096], P(('dp', 'tensor'))
- reduced: float32 [2048, 512], P('tensor', 'dp')
All inputs are finite; a program needn't handle non-finite values. No bound on the sum of `drop_mask` on one device may be relied on, other than what follows from the above.
Results may differ from a plain program's by a relative error of at most 0.012.
Values may be sent and summed in bfloat16 or wider, within the bound.
A program may use at most 128 MiB of HBM per device.

v0:
```python
import functools

import jax
import jax.numpy as jnp
from jax import lax
from jax.experimental import pallas as pl
from jax.experimental.pallas import tpu as pltpu
from jax.sharding import PartitionSpec as P

MESH = pl.DeviceIdType.MESH
F32 = jnp.float32
BF16 = jnp.bfloat16
FIRST = 8


def split(size, most, unit):
    parts = most
    while parts > 1 and (size % parts or (size // parts) % unit):
        parts -= 1
    return parts


def kernel(
    n, m, kc, gc, dc, first,
    tok, gain, wg, wu, wd, mask, grad,
    mixed, reduced,
    vg, vu, vd, gath, gain_v, mask_v, acc_g, acc_u, hid, part, pair, comb, recv, gown, grecv,
    w_sem, l_sem, gs_sem, gr_sem, fs_sem, as_sem, ar_sem, ps_sem, pr_sem, bs_sem, br_sem,
):
    me = lax.axis_index("tensor")
    my_dp = lax.axis_index("dp")
    rows, width = tok.shape
    ffl = wg.shape[1]
    kd, gd, cd = width // kc, width // gc, width // dc
    gcols = reduced.shape[1]
    par = lax.rem(me, 2)
    chip = lax.div(me, 2)
    sib = me + 1 - 2 * par
    half = n // 2

    weights = []
    for k in range(kc):
        r = pl.ds(k * kd, kd)
        weights.append(pltpu.make_async_copy(wg.at[r], vg.at[r], w_sem.at[2 * k]))
        weights.append(pltpu.make_async_copy(wu.at[r], vu.at[r], w_sem.at[2 * k + 1]))
    for c in range(dc):
        r = pl.ds(c * cd, cd)
        weights.append(pltpu.make_async_copy(wd.at[:, r], vd.at[:, r], w_sem.at[2 * kc + c]))

    tok_copy = pltpu.make_async_copy(tok, gath.at[me], l_sem.at[0])
    tok_copy.start()
    gain_copy = pltpu.make_async_copy(gain, gain_v, l_sem.at[1])
    gain_copy.start()
    mask_copy = pltpu.make_async_copy(mask, mask_v, l_sem.at[2])
    mask_copy.start()
    own_copy = pltpu.make_async_copy(grad.at[0, :, pl.ds(pl.multiple_of(my_dp * gcols, 128), gcols)], gown, l_sem.at[3])
    own_copy.start()
    barrier = pltpu.get_barrier_semaphore()
    for k in range(1, n):
        pl.semaphore_signal(barrier, inc=1, device_id={"tensor": lax.rem(me + k, n)}, device_id_type=MESH)
    for k in range(1, m):
        pl.semaphore_signal(barrier, inc=1, device_id={"dp": lax.rem(my_dp + k, m)}, device_id_type=MESH)
    for w in weights[:first]:
        w.start()
    tok_copy.wait()
    pl.semaphore_wait(barrier, n + m - 2)

    def rows_to(g, slot, peer, send_sem):
        c = pl.ds(g * gd, gd)
        return pltpu.make_async_remote_copy(
            src_ref=gath.at[slot, :, c], dst_ref=gath.at[slot, :, c], send_sem=send_sem, recv_sem=gr_sem.at[g, slot],
            device_id={"tensor": peer}, device_id_type=MESH)

    sends = []
    for g in range(gc):
        for k in list(range(1, half)) + [0]:
            peer = lax.rem(me + 2 * k, n) if k else sib
            sends.append(rows_to(g, me, peer, gs_sem.at[g, k]))
            sends[-1].start()
    later = weights[first:]
    for w in later[:4]:
        w.start()
    buckets = []
    for k in range(1, m):
        peer = lax.rem(my_dp + k, m)
        buckets.append(pltpu.make_async_remote_copy(
            src_ref=grad.at[0, :, pl.ds(pl.multiple_of(peer * gcols, 128), gcols)], dst_ref=grecv.at[k - 1],
            send_sem=bs_sem.at[k - 1], recv_sem=br_sem.at[k - 1], device_id={"dp": peer}, device_id_type=MESH))
        buckets[-1].start()
    gain_copy.wait()

    def forward(g):
        for k in range(1, half):
            slot = lax.rem(me + n - 2 * k, n)
            rows_to(g, slot, me, gs_sem.at[g, k]).wait_recv()
            sends.append(rows_to(g, slot, sib, fs_sem.at[g, k]))
            sends[-1].start()

    q = 8 // rows
    squares = [jnp.zeros((8, 1), F32) for _ in range(n // q)]
    forward(0)
    for w in later[4:]:
        w.start()
    for g in range(gc):
        if g + 1 < gc:
            forward(g + 1)
        for k in range(half):
            rows_to(g, lax.rem(sib + n - 2 * k, n), me, fs_sem.at[g, 0]).wait_recv()
        gains = gain_v[pl.ds(g * gd, gd)].astype(F32).reshape(1, gd)
        blocks = []
        for p in range(n // q):
            v = jnp.concatenate([gath[q * p + i, :, pl.ds(g * gd, gd)].astype(F32) for i in range(q)], axis=0)
            squares[p] = squares[p] + jnp.sum(v * v, axis=-1, keepdims=True)
            blocks.append(v * gains)
        xg = jnp.concatenate(blocks, axis=0).astype(BF16)
        for k in range(g * kc // gc, (g + 1) * kc // gc):
            r = pl.ds(k * kd, kd)
            xk = xg[:, k * kd - g * gd:(k + 1) * kd - g * gd]
            for j, (v, acc) in enumerate(((vg, acc_g), (vu, acc_u))):
                weights[2 * k + j].wait()
                d = jnp.dot(xk, v[r, :], preferred_element_type=F32)
                acc[...] = d if k == 0 else acc[...] + d

    scale = lax.rsqrt(jnp.concatenate(squares, axis=0) / width + 1e-05)
    gate = acc_g[...] * scale
    hid[...] = (gate / (1.0 + jnp.exp(-gate)) * (acc_u[...] * scale)).astype(BF16)

    h = hid[...]
    pairs, parts = [], []

    def combine(c):
        r = pl.ds(c * cd, cd)
        pairs[c].wait_recv()
        for j in range(half):
            comb[j, :, r] = (part[par, j, :, r].astype(F32) + pair[j, :, r].astype(F32)).astype(BF16)
        for k in range(1, half):
            to = lax.rem(chip + k, half)
            parts.append(pltpu.make_async_remote_copy(
                src_ref=comb.at[to, :, r], dst_ref=recv.at[k - 1, :, r],
                send_sem=ps_sem.at[c, k], recv_sem=pr_sem.at[c, k],
                device_id={"tensor": 2 * to + par}, device_id_type=MESH))
            parts[-1].start()

    for c in range(dc):
        r = pl.ds(c * cd, cd)
        weights[2 * kc + c].wait()
        d = jnp.dot(h, vd[:, r], preferred_element_type=F32)
        for j in range(n):
            part[j % 2, j // 2, :, r] = d[rows * j:rows * (j + 1), :].astype(BF16)
        pairs.append(pltpu.make_async_remote_copy(
            src_ref=part.at[1 - par, :, :, r], dst_ref=pair.at[:, :, r],
            send_sem=as_sem.at[c], recv_sem=ar_sem.at[c],
            device_id={"tensor": sib}, device_id_type=MESH))
        pairs[-1].start()
        if c:
            combine(c - 1)
    combine(dc - 1)

    own_copy.wait()
    for b in buckets:
        b.wait_recv()
    total = gown[...].astype(F32)
    for k in range(m - 1):
        total = total + grecv[k].astype(F32)
    reduced[...] = total

    mask_copy.wait()
    for c in range(dc):
        r = pl.ds(c * cd, cd)
        total = comb[chip, :, r].astype(F32)
        for k in range(1, half):
            parts[c * (half - 1) + k - 1].wait_recv()
            total = total + recv[k - 1, :, r].astype(F32)
        mixed[:, r] = (gath[me, :, r].astype(F32) + mask_v[:, r].astype(F32) * total / 0.9).astype(BF16)
    for s in sends + buckets + pairs + parts:
        s.wait_send()


def per_device(n, m, tokens, norm_gain, gate_weight, up_weight, down_weight, drop_mask, grad_bucket):
    rows, width = tokens.shape
    ffl = gate_weight.shape[1]
    grows, gcols = grad_bucket.shape[1], grad_bucket.shape[2] // m
    kc, gc, dc = split(width, 8, 128), split(width, 4, 128), split(width, 4, 128)
    half = n // 2
    hbm = pl.BlockSpec(memory_space=pl.ANY)
    dma = pltpu.SemaphoreType.DMA
    return pl.pallas_call(
        functools.partial(kernel, n, m, kc, gc, dc, FIRST),
        name="ffn",
        out_shape=(pltpu.VMEM((rows, width), BF16), pltpu.VMEM((grows, gcols), F32)),
        in_specs=[hbm] * 7,
        out_specs=(pl.BlockSpec(memory_space=pltpu.VMEM),) * 2,
        scratch_shapes=[
            pltpu.VMEM((width, ffl), BF16),
            pltpu.VMEM((width, ffl), BF16),
            pltpu.VMEM((ffl, width), BF16),
            pltpu.VMEM((n, rows, width), BF16),
            pltpu.VMEM((width,), BF16),
            pltpu.VMEM((rows, width), jnp.int32),
            pltpu.VMEM((n * rows, ffl), F32),
            pltpu.VMEM((n * rows, ffl), F32),
            pltpu.VMEM((n * rows, ffl), BF16),
            pltpu.VMEM((2, half, rows, width), BF16),
            pltpu.VMEM((half, rows, width), BF16),
            pltpu.VMEM((half, rows, width), BF16),
            pltpu.VMEM((half - 1, rows, width), BF16),
            pltpu.VMEM((grows, gcols), BF16),
            pltpu.VMEM((m - 1, grows, gcols), BF16),
            dma((2 * kc + dc,)), dma((4,)), dma((gc, half)), dma((gc, n)), dma((gc, half)),
            dma((dc,)), dma((dc,)), dma((dc, half)), dma((dc, half)), dma((m,)), dma((m,)),
        ],
        compiler_params=pltpu.CompilerParams(
            collective_id=0, has_side_effects=True, vmem_limit_bytes=56 * 2**20),
    )(tokens, norm_gain, gate_weight, up_weight, down_weight, drop_mask, grad_bucket)


def solution(mesh):
    return jax.shard_map(
        functools.partial(per_device, mesh.shape["tensor"], mesh.shape["dp"]),
        mesh=mesh,
        in_specs=(
            P(("dp", "tensor"), None),
            P(),
            P(None, "tensor"),
            P(None, "tensor"),
            P("tensor", None),
            P(("dp", "tensor"), None),
            P("dp", "tensor", None),
        ),
        out_specs=(P(("dp", "tensor"), None), P("tensor", "dp")),
        check_vma=False,
    )
```

profile of v0, /device:TPU:0, one launch (start us, length us, event | category | flops | bytes accessed | tf_op | source)
XLA Modules:
  0.0 26.6 jit_solution(15206388712780378300)
XLA Ops:
  0.6 24.7 %ffn.1 = (bf16[4,4096]{1,0:T(4,128)(2,1)S(1)}, f32[256,128]{1,0:T(8,128)S(1)}) custom-call(bf16[4,4096]{1,0:T(4,128)(2,1)} %tok.1, bf16[4096]{0:T(1024)(128)(2,1)} %gain.1, bf16[4096,1792]{1,0:T(8,128)(2,1)} %wg.1, bf16[4096,1792]{1,0:T(8,128)(2,1)} %wu.1, bf16[1792,4096]{1,0:T(8,128)(2,1)} %wd.1, s32[4,4096]{1,0:T(4,128)} %mask.1, bf16[1,256,512]{2,1,0:T(8,128)(2,1)} %grad.1), custom_call_target="tpu_custom_call" | custom-call | tf_op jit(solution)/shard_map/ffn/pallas_call | solution.py:187
  25.3 0.6 %copy.11 = bf16[4,4096]{1,0:T(4,128)(2,1)} copy(bf16[4,4096]{1,0:T(4,128)(2,1)S(1)} %get-tuple-element.2) | data formatting | bytes 65536
  25.9 0.7 %copy.12 = f32[256,128]{1,0:T(8,128)} copy(f32[256,128]{1,0:T(8,128)S(1)} %get-tuple-element.3) | data formatting | bytes 262144
where the time goes:
time: 26.7 us; the launch traced here: 26.6 us
  Pallas kernels  24.7 us (93%)
  local copies, waits for them, and re-layouts  1.27 us (5%)
  between operations  0.64 us (2%)
    pallas_call x1, Pallas kernels, per_device(): pl.pallas_call(functools.partial(kernel, n, m, kc, gc, dc, FIRST), name='...  24.7 us
    unnamed x2, local copies, waits for them, and re-layouts  1.27 us

commit v1 on v0

--- a/solution.py
+++ b/solution.py
@@ -21,6 +21,23 @@
 
 
 def kernel(
+    n, m, kc, gc, dc, first,
+    tok, gain, wg, wu, wd, mask, grad,
+    mixed, reduced,
+    vg, vu, vd, gath, gain_v, mask_v, acc_g, acc_u, hid, part, pair, comb, recv, gown, grecv,
+):
+    dma = pltpu.SemaphoreType.DMA
+    half = n // 2
+    pl.run_scoped(
+        functools.partial(
+            body, n, m, kc, gc, dc, first,
+            tok, gain, wg, wu, wd, mask, grad, mixed, reduced,
+            vg, vu, vd, gath, gain_v, mask_v, acc_g, acc_u, hid, part, pair, comb, recv, gown, grecv),
+        dma((2 * kc + dc,)), dma((4,)), dma((gc, half)), dma((gc, n)), dma((gc, half)),
+        dma((dc,)), dma((dc,)), dma((dc, half)), dma((dc, half)), dma((m,)), dma((m,)))
+
+
+def body(
     n, m, kc, gc, dc, first,
     tok, gain, wg, wu, wd, mask, grad,
     mixed, reduced,
@@ -176,15 +193,22 @@
         s.wait_send()
 
 
+def store(mixed, reduced, mixed_out, reduced_out, sem):
+    copies = [pltpu.make_async_copy(reduced, reduced_out, sem.at[0]), pltpu.make_async_copy(mixed, mixed_out, sem.at[1])]
+    for c in copies:
+        c.start()
+    for c in copies:
+        c.wait()
+
+
 def per_device(n, m, tokens, norm_gain, gate_weight, up_weight, down_weight, drop_mask, grad_bucket):
     rows, width = tokens.shape
     ffl = gate_weight.shape[1]
     grows, gcols = grad_bucket.shape[1], grad_bucket.shape[2] // m
-    kc, gc, dc = split(width, 8, 128), split(width, 4, 128), split(width, 4, 128)
+    kc, gc, dc = split(width, 4, 128), split(width, 4, 128), split(width, 4, 128)
     half = n // 2
     hbm = pl.BlockSpec(memory_space=pl.ANY)
-    dma = pltpu.SemaphoreType.DMA
-    return pl.pallas_call(
+    mixed, reduced = pl.pallas_call(
         functools.partial(kernel, n, m, kc, gc, dc, FIRST),
         name="ffn",
         out_shape=(pltpu.VMEM((rows, width), BF16), pltpu.VMEM((grows, gcols), F32)),
@@ -206,12 +230,19 @@
             pltpu.VMEM((half - 1, rows, width), BF16),
             pltpu.VMEM((grows, gcols), BF16),
             pltpu.VMEM((m - 1, grows, gcols), BF16),
-            dma((2 * kc + dc,)), dma((4,)), dma((gc, half)), dma((gc, n)), dma((gc, half)),
-            dma((dc,)), dma((dc,)), dma((dc, half)), dma((dc, half)), dma((m,)), dma((m,)),
         ],
         compiler_params=pltpu.CompilerParams(
             collective_id=0, has_side_effects=True, vmem_limit_bytes=56 * 2**20),
     )(tokens, norm_gain, gate_weight, up_weight, down_weight, drop_mask, grad_bucket)
+    return pl.pallas_call(
+        store,
+        name="store",
+        out_shape=(jax.ShapeDtypeStruct((rows, width), BF16), jax.ShapeDtypeStruct((grows, gcols), F32)),
+        in_specs=[pl.BlockSpec(memory_space=pltpu.VMEM)] * 2,
+        out_specs=(hbm, hbm),
+        scratch_shapes=[pltpu.SemaphoreType.DMA((2,))],
+        compiler_params=pltpu.CompilerParams(vmem_limit_bytes=2**20),
+    )(mixed, reduced)
 
 
 def solution(mesh):

time: 26.7 us -> 24.4 us (0.914)
  local copies, waits for them, and re-layouts: 1.27 us -> 0 us
  Pallas kernels: 24.7 us -> 23.6 us
    pallas_call x1, Pallas kernels: 24.7 us -> 22.9 us  [per_device(): pl.pallas_call(functools.partial(kernel, n, m, kc, gc, dc, FIRST), name='...]
    unnamed x2 -> x0, local copies, waits for them, and re-layouts: 1.27 us -> none
    pallas_call x0 -> x1, Pallas kernels: none -> 0.68 us  [per_device(): pl.pallas_call(store, name='store', out_shape=(jax.ShapeDtypeStruct((rows...]
where the time goes in v1:
time: 24.4 us; the launch traced here: 24.3 us
  Pallas kernels  23.6 us (97%)
  between operations  0.64 us (3%)
    pallas_call x1, Pallas kernels, per_device(): pl.pallas_call(functools.partial(kernel, n, m, kc, gc, dc, FIRST), name='...  22.9 us
    pallas_call x1, Pallas kernels, per_device(): pl.pallas_call(store, name='store', out_shape=(jax.ShapeDtypeStruct((rows...  0.68 us

profile of v1, /device:TPU:0, one launch (start us, length us, event | category | flops | bytes accessed | tf_op | source)
XLA Modules:
  0.0 24.3 jit_solution(925878252289516426)
XLA Ops:
  0.6 22.9 %ffn.1 = (bf16[4,4096]{1,0:T(4,128)(2,1)S(1)}, f32[256,128]{1,0:T(8,128)S(1)}) custom-call(bf16[4,4096]{1,0:T(4,128)(2,1)} %tok.1, bf16[4096]{0:T(1024)(128)(2,1)} %gain.1, bf16[4096,1792]{1,0:T(8,128)(2,1)} %wg.1, bf16[4096,1792]{1,0:T(8,128)(2,1)} %wu.1, bf16[1792,4096]{1,0:T(8,128)(2,1)} %wd.1, s32[4,4096]{1,0:T(4,128)} %mask.1, bf16[1,256,512]{2,1,0:T(8,128)(2,1)} %grad.1), custom_call_target="tpu_custom_call" | custom-call | tf_op jit(solution)/shard_map/ffn/pallas_call | solution.py:211
  23.6 0.7 %store.1 = (bf16[4,4096]{1,0:T(4,128)(2,1)}, f32[256,128]{1,0:T(8,128)}) custom-call(bf16[4,4096]{1,0:T(4,128)(2,1)S(1)} %get-tuple-element.4.mixed, f32[256,128]{1,0:T(8,128)S(1)} %get-tuple-element.5.reduced), custom_call_target="tpu_custom_call" | custom-call | tf_op jit(solution)/shard_map/store/pallas_call | solution.py:237

commit v2 on v1

--- a/solution.py
+++ b/solution.py
@@ -11,6 +11,10 @@
 F32 = jnp.float32
 BF16 = jnp.bfloat16
 FIRST = 8
+TILE = 256
+EARLY = 99
+LAG = 2
+DIRECT = 1
 
 
 def split(size, most, unit):
@@ -193,6 +197,298 @@
         s.wait_send()
 
 
+def mxu_kernel(
+    n, m, gc, dc,
+    tok, gain, wg, wu, wd, mask, grad,
+    mixed, reduced,
+    vg, vu, vd, gath, gain_v, mask_v, xs, hid, part, pair, comb, recv, dpart, drecv, gown, grecv,
+):
+    dma = pltpu.SemaphoreType.DMA
+    half, total_rows, tiles = n // 2, n * tok.shape[0], wg.shape[1] // TILE
+    acc = [pltpu.ACC(q)((total_rows, TILE), F32) for _ in range(tiles) for q in (0, 1)]
+    out = [pltpu.ACC(q)((total_rows, TILE), F32) for _ in range(wd.shape[1] // dc // TILE // 2) for q in (0, 1)]
+    pl.run_scoped(
+        functools.partial(
+            mxu_body, n, m, gc, dc,
+            tok, gain, wg, wu, wd, mask, grad, mixed, reduced,
+            vg, vu, vd, gath, gain_v, mask_v, xs, hid, part, pair, comb, recv, dpart, drecv, gown, grecv),
+        tuple(acc), tuple(out),
+        dma((2 * gc + dc,)), dma((4,)), dma((gc, half)), dma((gc, n)), dma((gc, half)), dma((gc, half)),
+        dma((dc,)), dma((dc,)), dma((dc, half)), dma((dc, half)), dma((n,)), dma((n,)), dma((m,)), dma((m,)))
+
+
+def mxu_body(
+    n, m, gc, dc,
+    tok, gain, wg, wu, wd, mask, grad,
+    mixed, reduced,
+    vg, vu, vd, gath, gain_v, mask_v, xs, hid, part, pair, comb, recv, dpart, drecv, gown, grecv,
+    acc, out,
+    w_sem, l_sem, gs_sem, gr_sem, fs_sem, fr_sem, as_sem, ar_sem, ps_sem, pr_sem, ds_sem, dr_sem, bs_sem, br_sem,
+):
+    me = lax.axis_index("tensor")
+    my_dp = lax.axis_index("dp")
+    rows, width = tok.shape
+    ffl = wg.shape[1]
+    gd, cd = width // gc, width // dc
+    gcols = reduced.shape[1]
+    par = lax.rem(me, 2)
+    chip = lax.div(me, 2)
+    sib = me + 1 - 2 * par
+    half = n // 2
+    tiles, kb_g, kb_d = ffl // TILE, gd // TILE, ffl // TILE
+    step = 2 * lax.div(chip, half // 2) - 1
+    scope = jax.named_scope
+
+    def far(i):
+        return lax.rem(chip + step * i + half, half)
+
+    tok_copy = pltpu.make_async_copy(tok, gath.at[me], l_sem.at[0])
+    tok_copy.start()
+    gain_copy = pltpu.make_async_copy(gain, gain_v, l_sem.at[1])
+    gain_copy.start()
+    mask_copy = pltpu.make_async_copy(mask, mask_v, l_sem.at[2])
+    mask_copy.start()
+    own_copy = pltpu.make_async_copy(grad.at[0, :, pl.ds(pl.multiple_of(my_dp * gcols, 128), gcols)], gown, l_sem.at[3])
+    own_copy.start()
+    barrier = pltpu.get_barrier_semaphore()
+    for k in range(1, n):
+        pl.semaphore_signal(barrier, inc=1, device_id={"tensor": lax.rem(me + k, n)}, device_id_type=MESH)
+    for k in range(1, m):
+        pl.semaphore_signal(barrier, inc=1, device_id={"dp": lax.rem(my_dp + k, m)}, device_id_type=MESH)
+    weights = []
+    for g in range(gc):
+        r = pl.ds(g * gd, gd)
+        weights.append(pltpu.make_async_copy(wg.at[r], vg.at[r], w_sem.at[2 * g]))
+        weights.append(pltpu.make_async_copy(wu.at[r], vu.at[r], w_sem.at[2 * g + 1]))
+    for c in range(dc):
+        r = pl.ds(c * cd, cd)
+        weights.append(pltpu.make_async_copy(wd.at[:, r], vd.at[:, r], w_sem.at[2 * gc + c]))
+    for w in weights[:EARLY]:
+        w.start()
+    with scope("tok"):
+        tok_copy.wait()
+    with scope("barrier"):
+        pl.semaphore_wait(barrier, n + m - 2)
+
+    def rows_to(g, slot, peer, send_sem):
+        c = pl.ds(g * gd, gd)
+        return pltpu.make_async_remote_copy(
+            src_ref=gath.at[slot, :, c], dst_ref=gath.at[slot, :, c], send_sem=send_sem, recv_sem=gr_sem.at[g, slot],
+            device_id={"tensor": peer}, device_id_type=MESH)
+
+    def chip_to(g, q):
+        c, r = pl.ds(g * gd, gd), pl.ds(2 * q, 2)
+        return pltpu.make_async_remote_copy(
+            src_ref=gath.at[r, :, c], dst_ref=gath.at[r, :, c], send_sem=fs_sem.at[g, q], recv_sem=fr_sem.at[g, q],
+            device_id={"tensor": sib}, device_id_type=MESH)
+
+    sends = []
+    for g in range(gc):
+        for i in range(1, half):
+            sends.append(rows_to(g, me, 2 * far(i) + 1, gs_sem.at[g, i]))
+            sends[-1].start()
+        sends.append(rows_to(g, me, sib, gs_sem.at[g, 0]))
+        sends[-1].start()
+    for w in weights[EARLY:]:
+        w.start()
+    buckets = []
+    for k in range(1, m):
+        peer = lax.rem(my_dp + k, m)
+        buckets.append(pltpu.make_async_remote_copy(
+            src_ref=grad.at[0, :, pl.ds(pl.multiple_of(peer * gcols, 128), gcols)], dst_ref=grecv.at[k - 1],
+            send_sem=bs_sem.at[k - 1], recv_sem=br_sem.at[k - 1], device_id={"dp": peer}, device_id_type=MESH))
+        buckets[-1].start()
+    gain_copy.wait()
+
+    def gather(g):
+        with scope(f"gather{g}"):
+            @pl.when(par == 1)
+            def _():
+                for i in range(half - 1, 0, -1):
+                    q = far(i)
+                    for p in range(2):
+                        rows_to(g, 2 * q + p, me, gs_sem.at[g, i]).wait_recv()
+                    chip_to(g, q).start()
+
+            @pl.when(par == 0)
+            def _():
+                for i in range(half - 1, 0, -1):
+                    chip_to(g, far(i)).wait_recv()
+            rows_to(g, sib, me, gs_sem.at[g, 0]).wait_recv()
+
+    per = 8 // rows
+    groups = [[2 * (per * b + i) + p for i in range(per)] for p in range(2) for b in range(half // per)]
+    squares = [jnp.zeros((8, 1), F32) for _ in groups]
+
+    def norm(g):
+        c = pl.ds(g * gd, gd)
+        gains = gain_v[c].astype(F32).reshape(1, gd)
+        blocks = []
+        for b, slots in enumerate(groups):
+            v = jnp.concatenate([gath[s, :, c].astype(F32) for s in slots], axis=0)
+            squares[b] = squares[b] + jnp.sum(v * v, axis=-1, keepdims=True)
+            blocks.append(v * gains)
+        xs[:, c] = jnp.concatenate(blocks, axis=0).astype(BF16)
+
+    turn = [0, 0]
+
+    def multiply(q, to, left, right):
+        pltpu.matmul_push_rhs(right, staging_register=turn[q], mxu_index=q)
+        pltpu.matmul_acc_lhs(to, left, load_staged_rhs=turn[q])
+        turn[q] = 1 - turn[q]
+
+    def activate(t, scale):
+        gate = pltpu.matmul_pop(acc[2 * t]) * scale
+        up = pltpu.matmul_pop(acc[2 * t + 1]) * scale
+        hid[:, pl.ds(t * TILE, TILE)] = (gate / (1.0 + jnp.exp(-gate)) * up).astype(BF16)
+
+    gather(0)
+    norm(0)
+    scale = None
+    for g in range(gc):
+        with scope(f"w{g}"):
+            weights[2 * g].wait()
+            weights[2 * g + 1].wait()
+        last = g == gc - 1
+        if last:
+            scale = lax.rsqrt(jnp.concatenate(squares, axis=0) / width + 1e-05)
+        for t in range(tiles):
+            f = pl.ds(t * TILE, TILE)
+            for k in range(kb_g):
+                r = pl.ds(g * gd + k * TILE, TILE)
+                multiply(0, acc[2 * t], xs[:, r], vg[r, f])
+                multiply(1, acc[2 * t + 1], xs[:, r], vu[r, f])
+            if last and t:
+                activate(t - 1, scale)
+            if not last and t == tiles // 2:
+                gather(g + 1)
+                norm(g + 1)
+
+    pairs, parts = [], []
+
+    def combine(c):
+        r = pl.ds(c * cd, cd)
+        with scope(f"pair{c}"):
+            pairs[c].wait_recv()
+        both = part[par, :, r].astype(F32) + pair[:, r].astype(F32)
+        for j in range(half):
+            comb[j, :, r] = both[rows * j:rows * (j + 1), :].astype(BF16)
+        for i in range(1, half):
+            to = far(i)
+            parts.append(pltpu.make_async_remote_copy(
+                src_ref=comb.at[to, :, r], dst_ref=recv.at[chip, :, r],
+                send_sem=ps_sem.at[c, i], recv_sem=pr_sem.at[c, chip],
+                device_id={"tensor": 2 * to + par}, device_id_type=MESH))
+            parts[-1].start()
+
+    def part_of(c, q):
+        r = pl.ds(c * cd, cd)
+        return pltpu.make_async_remote_copy(
+            src_ref=comb.at[q, :, r], dst_ref=recv.at[q, :, r],
+            send_sem=ps_sem.at[c, 0], recv_sem=pr_sem.at[c, q],
+            device_id={"tensor": sib}, device_id_type=MESH)
+
+    def slot_to(slot, peer, i):
+        return pltpu.make_async_remote_copy(
+            src_ref=dpart.at[peer], dst_ref=drecv.at[slot],
+            send_sem=ds_sem.at[i], recv_sem=dr_sem.at[slot],
+            device_id={"tensor": peer}, device_id_type=MESH)
+
+    half_rows = half * rows
+    directs = []
+    for c in range(dc):
+        with scope(f"wd{c}"):
+            weights[2 * gc + c].wait()
+        pair_tiles = cd // TILE // 2
+        for k in range(kb_d):
+            if c == 0 and k == kb_d - 1:
+                activate(tiles - 1, scale)
+            r = pl.ds(k * TILE, TILE)
+            for t in range(pair_tiles):
+                for q in range(2):
+                    multiply(q, out[2 * t + q], hid[:, r], vd[r, pl.ds(c * cd + (2 * t + q) * TILE, TILE)])
+        for t in range(2 * pair_tiles):
+            d = pltpu.matmul_pop(out[t])
+            if c < dc - DIRECT:
+                for p in range(2):
+                    part[p, :, pl.ds(c * cd + t * TILE, TILE)] = d[p * half_rows:(p + 1) * half_rows, :].astype(BF16)
+            else:
+                for s in range(n):
+                    at = (s % 2) * half_rows + (s // 2) * rows
+                    dpart[s, :, pl.ds(t * TILE, TILE)] = d[at:at + rows, :].astype(BF16)
+        if c < dc - DIRECT:
+            r = pl.ds(c * cd, cd)
+            pairs.append(pltpu.make_async_remote_copy(
+                src_ref=part.at[1 - par, :, r], dst_ref=pair.at[:, r],
+                send_sem=as_sem.at[c], recv_sem=ar_sem.at[c],
+                device_id={"tensor": sib}, device_id_type=MESH))
+            pairs[-1].start()
+        else:
+            for i in range(1, half):
+                for p in range(2):
+                    directs.append(slot_to(me, 2 * far(i) + p, 2 * i + p))
+                    directs[-1].start()
+            directs.append(slot_to(me, sib, 0))
+            directs[-1].start()
+        if c >= LAG and c - LAG < dc - DIRECT:
+            combine(c - LAG)
+        if c == dc // 2:
+            with scope("bucket"):
+                own_copy.wait()
+                for b in buckets:
+                    b.wait_recv()
+            total = gown[...].astype(F32)
+            for k in range(m - 1):
+                total = total + grecv[k].astype(F32)
+            reduced[...] = total
+    for c in range(len(parts) // (half - 1), dc - DIRECT):
+        combine(c)
+
+    mask_copy.wait()
+
+    def finish(c, total):
+        r = pl.ds(c * cd, cd)
+        mixed[:, r] = (gath[me, :, r].astype(F32) + mask_v[:, r].astype(F32) * total / 0.9).astype(BF16)
+
+    for c in range(dc - DIRECT):
+        r = pl.ds(c * cd, cd)
+        total = comb[chip, :, r].astype(F32)
+        with scope(f"part{c}"):
+            for i in range(1, half):
+                part_of(c, far(i)).wait_recv()
+        for i in range(1, half):
+            total = total + recv[far(i), :, r].astype(F32)
+        finish(c, total)
+    if DIRECT:
+        total = dpart[me].astype(F32)
+        with scope("direct"):
+            slot_to(sib, me, 0).wait_recv()
+            for i in range(half - 1, 0, -1):
+                for p in range(2):
+                    slot_to(2 * far(i) + p, me, 0).wait_recv()
+        total = total + drecv[sib].astype(F32)
+        for i in range(1, half):
+            for p in range(2):
+                total = total + drecv[2 * far(i) + p].astype(F32)
+        finish(dc - 1, total)
+    with scope("sent"):
+        for s in sends + buckets + pairs + parts + directs:
+            s.wait_send()
+
+        @pl.when(par == 1)
+        def _():
+            for g in range(gc):
+                for i in range(1, half):
+                    chip_to(g, far(i)).wait_send()
+
+
+def mxu_fits(n, rows, width, ffl):
+    count = n * rows
+    entries = count // 4 * (ffl // TILE + width // (8 * TILE))
+    return (ffl % TILE == 0 and width % (16 * TILE) == 0 and count % 16 == 0 and 8 % rows == 0
+            and n % 4 == 0 and (n // 2) * rows % 8 == 0 and entries <= 256)
+
+
 def store(mixed, reduced, mixed_out, reduced_out, sem):
     copies = [pltpu.make_async_copy(reduced, reduced_out, sem.at[0]), pltpu.make_async_copy(mixed, mixed_out, sem.at[1])]
     for c in copies:
@@ -208,19 +504,31 @@
     kc, gc, dc = split(width, 4, 128), split(width, 4, 128), split(width, 4, 128)
     half = n // 2
     hbm = pl.BlockSpec(memory_space=pl.ANY)
-    mixed, reduced = pl.pallas_call(
-        functools.partial(kernel, n, m, kc, gc, dc, FIRST),
-        name="ffn",
-        out_shape=(pltpu.VMEM((rows, width), BF16), pltpu.VMEM((grows, gcols), F32)),
-        in_specs=[hbm] * 7,
-        out_specs=(pl.BlockSpec(memory_space=pltpu.VMEM),) * 2,
-        scratch_shapes=[
-            pltpu.VMEM((width, ffl), BF16),
-            pltpu.VMEM((width, ffl), BF16),
-            pltpu.VMEM((ffl, width), BF16),
-            pltpu.VMEM((n, rows, width), BF16),
-            pltpu.VMEM((width,), BF16),
-            pltpu.VMEM((rows, width), jnp.int32),
+    common = [
+        pltpu.VMEM((width, ffl), BF16),
+        pltpu.VMEM((width, ffl), BF16),
+        pltpu.VMEM((ffl, width), BF16),
+        pltpu.VMEM((n, rows, width), BF16),
+        pltpu.VMEM((width,), BF16),
+        pltpu.VMEM((rows, width), jnp.int32),
+    ]
+    bucket = [pltpu.VMEM((grows, gcols), BF16), pltpu.VMEM((m - 1, grows, gcols), BF16)]
+    if mxu_fits(n, rows, width, ffl):
+        dc = split(width, 8, 2 * TILE)
+        body = functools.partial(mxu_kernel, n, m, gc, dc)
+        scratch = common + [
+            pltpu.VMEM((n * rows, width), BF16),
+            pltpu.VMEM((n * rows, ffl), BF16),
+            pltpu.VMEM((2, half * rows, width), BF16),
+            pltpu.VMEM((half * rows, width), BF16),
+            pltpu.VMEM((half, rows, width), BF16),
+            pltpu.VMEM((half, rows, width), BF16),
+            pltpu.VMEM((n, rows, width // dc), BF16),
+            pltpu.VMEM((n, rows, width // dc), BF16),
+        ] + bucket
+    else:
+        body = functools.partial(kernel, n, m, kc, gc, dc, FIRST)
+        scratch = common + [
             pltpu.VMEM((n * rows, ffl), F32),
             pltpu.VMEM((n * rows, ffl), F32),
             pltpu.VMEM((n * rows, ffl), BF16),
@@ -228,9 +536,14 @@
             pltpu.VMEM((half, rows, width), BF16),
             pltpu.VMEM((half, rows, width), BF16),
             pltpu.VMEM((half - 1, rows, width), BF16),
-            pltpu.VMEM((grows, gcols), BF16),
-            pltpu.VMEM((m - 1, grows, gcols), BF16),
-        ],
+        ] + bucket
+    mixed, reduced = pl.pallas_call(
+        body,
+        name="ffn",
+        out_shape=(pltpu.VMEM((rows, width), BF16), pltpu.VMEM((grows, gcols), F32)),
+        in_specs=[hbm] * 7,
+        out_specs=(pl.BlockSpec(memory_space=pltpu.VMEM),) * 2,
+        scratch_shapes=scratch,
         compiler_params=pltpu.CompilerParams(
             collective_id=0, has_side_effects=True, vmem_limit_bytes=56 * 2**20),
     )(tokens, norm_gain, gate_weight, up_weight, down_weight, drop_mask, grad_bucket)

time: 24.4 us -> 23.9 us (0.980)
  Pallas kernels: 23.6 us -> 23.1 us
    pallas_call x1, Pallas kernels: 22.9 us -> 22.4 us  [per_device(): pl.pallas_call(body, name='ffn', out_shape=(pltpu.VMEM((rows, width), BF1...]
where the time goes in v2:
time: 23.9 us; the launch traced here: 23.8 us
  Pallas kernels  23.1 us (97%)
  between operations  0.64 us (3%)
    pallas_call x1, Pallas kernels, per_device(): pl.pallas_call(body, name='ffn', out_shape=(pltpu.VMEM((rows, width), BF1...  22.4 us
    pallas_call x1, Pallas kernels, per_device(): pl.pallas_call(store, name='store', out_shape=(jax.ShapeDtypeStruct((rows...  0.68 us

profile of v2, /device:TPU:0, one launch (start us, length us, event | category | flops | bytes accessed | tf_op | source)
XLA Modules:
  0.0 23.8 jit_solution(7894304220908036468)
XLA Ops:
  0.6 22.4 %ffn.1 = (bf16[4,4096]{1,0:T(4,128)(2,1)S(1)}, f32[256,128]{1,0:T(8,128)S(1)}) custom-call(bf16[4,4096]{1,0:T(4,128)(2,1)} %tok.1, bf16[4096]{0:T(1024)(128)(2,1)} %gain.1, bf16[4096,1792]{1,0:T(8,128)(2,1)} %wg.1, bf16[4096,1792]{1,0:T(8,128)(2,1)} %wu.1, bf16[1792,4096]{1,0:T(8,128)(2,1)} %wd.1, s32[4,4096]{1,0:T(4,128)} %mask.1, bf16[1,256,512]{2,1,0:T(8,128)(2,1)} %grad.1), custom_call_target="tpu_custom_call" | custom-call | tf_op jit(solution)/shard_map/ffn/pallas_call | solution.py:540
  23.1 0.7 %store.1 = (bf16[4,4096]{1,0:T(4,128)(2,1)}, f32[256,128]{1,0:T(8,128)}) custom-call(bf16[4,4096]{1,0:T(4,128)(2,1)S(1)} %get-tuple-element.4.mixed, f32[256,128]{1,0:T(8,128)S(1)} %get-tuple-element.5.reduced), custom_call_target="tpu_custom_call" | custom-call | tf_op jit(solution)/shard_map/store/pallas_call | solution.py:550
